TPU v7x, 32 devices: a whole 2x2x4 slice. The times are simulated.
32 devices in a mesh: wide: 16 (over z, y, core), narrow: 2 (over x).
Axes of the slice: x: 2, y: 2, z: 4, core: 2. Of those that a mesh axis runs over, the one named last changes fastest.
Arguments:
- gradient: float32 [3072, 3072], P('wide', 'narrow'), may hold values from -6 to 6
- first_moment: float32 [3072, 3072], P('wide', 'narrow'), may hold values from -6 to 6
- second_moment: float32 [3072, 3072], P('wide', 'narrow'), may hold values from 0.25 to 4
- left_basis: float32 [3072, 3072], P('wide', 'narrow'), may hold values from -0.15625 to 0.15625
- right_basis: float32 [3072, 3072], P('wide', 'narrow'), may hold values from -0.109375 to 0.109375
Outputs:
- update: float32 [3072, 3072], P('wide', 'narrow')
- new_first: float32 [3072, 3072], P('wide', 'narrow')
- new_second: float32 [3072, 3072], P('wide', 'narrow')
All inputs are finite; a program needn't handle non-finite values.
Results may differ from a plain program's by a relative error of at most 0.000075.
Values sent between devices are 32-bit elements; how exact they have to be, the bound alone decides.
A program may use at most 128 MiB of HBM per device.

v0:
```python
import jax
import jax.numpy as jnp
from jax import lax
from jax.sharding import PartitionSpec as P

STEP = 10
beta_first = 0.9
beta_second = 0.95
epsilon = 1e-08


def product(left, right):
    return jnp.dot(left, right, precision=lax.Precision.HIGHEST, preferred_element_type=jnp.float32)


def contract(left, right, left_dim, right_dim):
    return lax.dot_general(
        left,
        right,
        (((left_dim,), (right_dim,)), ((), ())),
        precision=lax.Precision.HIGHEST,
        preferred_element_type=jnp.float32,
    )


def body(gradient, first_moment, second_moment, left_basis, right_basis):
    grad_rows, left_rows = (
        lax.all_gather(gradient, "narrow", axis=1, tiled=True),
        lax.all_gather(left_basis, "narrow", axis=1, tiled=True),
    )
    columns = grad_rows
    rotated_right = product(columns, lax.all_gather(right_basis, "wide", axis=0, tiled=True))
    columns = left_rows
    rotated = lax.psum_scatter(
        contract(columns, rotated_right, 0, 0), "wide", scatter_dimension=0, tiled=True
    )
    new_first = beta_first * first_moment + (1.0 - beta_first) * rotated
    new_second = beta_second * second_moment + (1.0 - beta_second) * rotated * rotated
    direction = (
        new_first
        / (1.0 - beta_first**STEP)
        / (jnp.sqrt(new_second / (1.0 - beta_second**STEP)) + epsilon)
    )
    columns = left_rows
    back_left = product(columns, lax.all_gather(direction, "wide", axis=0, tiled=True))
    terms = contract(back_left, lax.all_gather(right_basis, "wide", axis=0, tiled=True), 1, 1)
    update = lax.psum_scatter(terms, "narrow", scatter_dimension=1, tiled=True)
    return (update, new_first, new_second)


def solution(mesh):
    placed = (
        P("wide", "narrow"),
        P("wide", "narrow"),
        P("wide", "narrow"),
        P("wide", "narrow"),
        P("wide", "narrow"),
    )
    return jax.shard_map(
        body,
        mesh=mesh,
        in_specs=placed,
        out_specs=(P("wide", "narrow"), P("wide", "narrow"), P("wide", "narrow")),
        check_vma=False,
    )
```

profile of v0, /device:TPU:0, one launch (start us, length us, event | category | flops | bytes accessed | tf_op | source)
XLA Modules:
  0.0 637.2 jit_solution(4374816837675824320)
XLA Ops:
  7.2 0.7 all-gather.5.cloned.1.call-update
  7.9 0.7 all-gather.7.cloned.1.call-update
  8.7 0.7 all-gather.9.cloned.1.call-update
  9.4 38.9 %all-gather.5.cloned.1.call-done = f32[192,3072]{1,0:T(8,128)} async-done(((f32[192,1536]{1,0:T(8,128)}), f32[192,3072]{1,0:T(8,128)}) %all-gather.5.cloned.1.call-update) | async-done | bytes 2359312 | tf_op jit(solution)/shard_map/all_gather | solution.py:28
  48.3 100.5 %all-gather.7.cloned.1.call-done = f32[3072,1536]{1,0:T(8,128)} async-done(((f32[192,1536]{1,0:T(8,128)}), f32[3072,1536]{1,0:T(8,128)}) %all-gather.7.cloned.1.call-update) | async-done | bytes 18874384 | tf_op jit(solution)/shard_map/all_gather | solution.py:32
  148.8 16.6 %fusion.2 = f32[192,1536]{1,0:T(8,128)S(1)} fusion(f32[192,3072]{1,0:T(8,128)} %all-gather.5.cloned.1.call-done, f32[3072,1536]{1,0:T(8,128)} %all-gather.7.cloned.1.call-done), kind=kOutput, calls=%fused_computation.5 | convolution fusion | flops 10871635968 | bytes 22413312 | tf_op jit(solution)/shard_map/dot_general | solution.py:13
  165.5 21.0 %all-gather.9.cloned.1.call-done = f32[192,3072]{1,0:T(8,128)} async-done(((f32[192,1536]{1,0:T(8,128)}), f32[192,3072]{1,0:T(8,128)}) %all-gather.9.cloned.1.call-update) | async-done | bytes 2359312 | tf_op jit(solution)/shard_map/all_gather | solution.py:29
  186.5 19.5 %convolution_bitcast_fusion = f32[3072,1536]{0,1:T(8,128)} fusion(f32[192,1536]{1,0:T(8,128)S(1)} %fusion.2, f32[192,3072]{1,0:T(8,128)} %all-gather.9.cloned.1.call-done), kind=kOutput, calls=%fused_computation | convolution fusion | flops 10871635968 | bytes 22413312 | tf_op jit(solution)/shard_map/dot_general | solution.py:17
  206.0 18.7 %copy.17 = f32[3072,1536]{1,0:T(8,128)} copy(f32[3072,1536]{0,1:T(8,128)} %convolution_bitcast_fusion) | data formatting | bytes 37748736
  224.7 0.2 all-gather.11.cloned.1.call-start
  225.0 1.0 copy-done.3
  226.0 0.5 copy.12
  226.4 1.7 copy.13
  228.2 190.7 %reduce-scatter.7.cloned.1.call-done = f32[192,1536]{1,0:T(8,128)} async-done(((f32[3072,1536]{1,0:T(8,128)}), f32[192,1536]{1,0:T(8,128)}) %reduce-scatter.7.cloned.1.call-update) | async-done | bytes 1179664
  418.9 3.0 copy.18
  421.9 4.1 add_divide_fusion
  426.0 3.0 copy.14
  429.1 98.1 %all-gather.11.cloned.1.call-done = f32[3072,1536]{1,0:T(8,128)} async-done(((f32[192,1536]{1,0:T(8,128)}), f32[3072,1536]{1,0:T(8,128)}) %all-gather.11.cloned.1.call-update) | async-done | bytes 18874384 | tf_op jit(solution)/shard_map/all_gather | solution.py:45
  527.2 32.5 %fusion.3 = f32[1536,192]{1,0:T(8,128)S(1)} fusion(f32[3072,1536]{1,0:T(8,128)} %all-gather.11.cloned.1.call-done, f32[192,3072]{1,0:T(8,128)S(1)} %copy-done), kind=kOutput, calls=%fused_computation.6 | convolution fusion | flops 10871635968 | bytes 22413312 | tf_op jit(solution)/shard_map/dot_general | solution.py:13
  559.8 35.7 %fusion.4 = f32[192,3072]{1,0:T(8,128)} fusion(f32[1536,192]{1,0:T(8,128)S(1)} %fusion.3, f32[3072,1536]{1,0:T(8,128)} %all-gather.7.cloned.1.call-done), kind=kOutput, calls=%fused_computation.7 | convolution fusion | flops 10871635968 | bytes 22413312 | tf_op jit(solution)/shard_map/dot_general | solution.py:17
  595.5 1.4 copy-done.2
  596.8 1.5 copy.15
  598.3 1.5 copy.16
  599.8 30.6 %reduce-scatter.5.cloned.1.call-done = f32[192,1536]{1,0:T(8,128)} async-done(((f32[192,3072]{1,0:T(8,128)}), f32[192,1536]{1,0:T(8,128)}) %reduce-scatter.5.cloned.1.call-update) | async-done | bytes 1179664 | tf_op jit(solution)/shard_map/reduce_scatter | solution.py:47
  (14 shorter events, 0.3 us)
Async XLA Ops:
  7.2 41.2 %all-gather.5.cloned.1.call-start = ((), (), s32[]{:S(2)}) async-start(), calls=%async_computation.2 | async-start | bytes 3538944 | tf_op jit(solution)/shard_map/all_gather | solution.py:28
  7.9 140.9 %all-gather.7.cloned.1.call-start = ((), (), s32[]{:S(2)}) async-start(), calls=%async_computation.3 | async-start | bytes 20054016 | tf_op jit(solution)/shard_map/all_gather | solution.py:32
  8.6 177.8 %all-gather.9.cloned.1.call-start = ((), (), s32[]{:S(2)}) async-start(), calls=%async_computation.4 | async-start | bytes 3538944 | tf_op jit(solution)/shard_map/all_gather | solution.py:29
  9.4 409.5 %reduce-scatter.7.cloned.1.call-start = ((), (), s32[]{:S(2)}) async-start(), calls=%async_computation.7 | async-start | bytes 20054016
  224.7 1.3 copy-start.3
  224.7 302.5 %all-gather.11.cloned.1.call-start = ((), (), s32[]{:S(2)}) async-start(), calls=%async_computation.5 | async-start | bytes 20054016 | tf_op jit(solution)/shard_map/all_gather | solution.py:45
  426.0 101.2 %copy-start = (f32[192,3072]{1,0:T(8,128)S(1)}, f32[192,3072]{1,0:T(8,128)}, u32[]{:S(2)}) copy-start(f32[192,3072]{1,0:T(8,128)} %all-gather.9.cloned.1.call-done) | copy-start | bytes 7077892
  429.1 201.3 %reduce-scatter.5.cloned.1.call-start = ((), (), s32[]{:S(2)}) async-start(), calls=%async_computation.6 | async-start | bytes 3538944 | tf_op jit(solution)/shard_map/reduce_scatter | solution.py:47
  595.4 1.4 copy-start.2
  595.5 2.9 copy-start.1
Sparse Core Ops, SparseCore 0:
  9.5 38.7 all-gather.4
  49.9 98.8 all-gather.6
  150.4 36.0 all-gather.8
  224.9 194.0 reduce-scatter.6
  429.2 98.0 all-gather.10
  595.6 34.7 reduce-scatter.4
where the time goes:
time: 638 us; the launch traced here: 637 us
  waiting for transfers between devices  482 us (76%)
  matrix products  104 us (16%)
  local copies, waits for them, and re-layouts  32.2 us (5%)
  between operations  14.2 us (2%)
    unnamed x7, waiting for transfers between devices  193 us
    all_gather x1, waiting for transfers between devices, body(): lax.all_gather(right_basis, 'wide', axis=0, tiled=True)  101 us
    all_gather x1, waiting for transfers between devices, body(): lax.all_gather(direction, 'wide', axis=0, tiled=True)  98.1 us
    dot_general x2, matrix products, contract(): lax.dot_general(left, right, (((left_dim,), (right_dim,)), ((), ())), pre...  55.2 us
    dot_general x2, matrix products, product(): jnp.dot(left, right, precision=lax.Precision.HIGHEST, preferred_element_t...  49.1 us
    all_gather x1, waiting for transfers between devices, body(): lax.all_gather(gradient, 'narrow', axis=1, tiled=True)  38.9 us
    reduce_scatter x1, waiting for transfers between devices, body(): update = lax.psum_scatter(terms, 'narrow', scatter_dimension=1, tiled=True)  30.6 us
    unnamed x14, local copies, waits for them, and re-layouts  29.2 us
  transfers between devices with their start and end apart: 6, of which 6 were waited for; matrix products, arithmetic and copies ran while one was open for 3% of the time, Pallas kernels for 0%

commit v1 on v0

--- a/solution.py
+++ b/solution.py
@@ -25,7 +25,7 @@
 
 def body(gradient, first_moment, second_moment, left_basis, right_basis):
     grad_rows, left_rows = (
-        lax.all_gather(gradient, "narrow", axis=1, tiled=True),
+        jnp.concatenate(lax.all_gather(gradient, "narrow"), axis=1),
         lax.all_gather(left_basis, "narrow", axis=1, tiled=True),
     )
     columns = grad_rows

time: 638 us -> 609 us (0.955)
  matrix products: 104 us -> 75.1 us
    dot_general x2, matrix products: 49.1 us -> 32.5 us  [product(): jnp.dot(left, right, precision=lax.Precision.HIGHEST, preferred_element_t...]
    dot_general x2, matrix products: 55.2 us -> 42.6 us  [contract(): lax.dot_general(left, right, (((left_dim,), (right_dim,)), ((), ())), pre...]
    unnamed x14 -> x15, local copies, waits for them, and re-layouts: 29.2 us -> 29.6 us
  transfers between devices with their start and end apart: 6 -> 6, of which waited for: 6 -> 6; matrix products, arithmetic and copies ran while one was open for 3% -> 4% of each run, Pallas kernels for 0% -> 0%
where the time goes in v1:
time: 609 us
  waiting for transfers between devices  479 us (79%)
  matrix products  75.1 us (12%)
  local copies, waits for them, and re-layouts  36.1 us (6%)
  between operations  14.2 us (2%)
    unnamed x7, waiting for transfers between devices  193 us
    all_gather x1, waiting for transfers between devices, body(): lax.all_gather(direction, 'wide', axis=0, tiled=True)  98.1 us
    all_gather x1, waiting for transfers between devices, body(): lax.all_gather(right_basis, 'wide', axis=0, tiled=True)  96.6 us
    dot_general x2, matrix products, contract(): lax.dot_general(left, right, (((left_dim,), (right_dim,)), ((), ())), pre...  42.6 us
    all_gather x1, waiting for transfers between devices, body(): lax.all_gather(gradient, 'narrow')  38.9 us
    dot_general x2, matrix products, product(): jnp.dot(left, right, precision=lax.Precision.HIGHEST, preferred_element_t...  32.5 us
    reduce_scatter x1, waiting for transfers between devices, body(): update = lax.psum_scatter(terms, 'narrow', scatter_dimension=1, tiled=True)  30.6 us
    unnamed x15, local copies, waits for them, and re-layouts  29.6 us
  transfers between devices with their start and end apart: 6, of which 6 were waited for; matrix products, arithmetic and copies ran while one was open for 4% of the time, Pallas kernels for 0%

profile of v1, /device:TPU:0, one launch (start us, length us, event | category | flops | bytes accessed | tf_op | source)
XLA Modules:
  0.0 608.7 jit_solution(17895347504615176625)
XLA Ops:
  7.2 0.7 all-gather.12.cloned.1.call-update
  7.9 0.7 all-gather.6.cloned.1.call-update
  8.7 0.7 all-gather.8.cloned.1.call-update
  9.4 38.9 %all-gather.12.cloned.1.call-done = f32[384,1536]{1,0:T(8,128)} async-done(((f32[192,1536]{1,0:T(8,128)}), f32[384,1536]{1,0:T(8,128)}) %all-gather.12.cloned.1.call-update) | async-done | bytes 2359312 | tf_op jit(solution)/shard_map/all_gather | solution.py:28
  48.3 3.5 copy.18
  52.2 96.6 %all-gather.6.cloned.1.call-done = f32[3072,1536]{1,0:T(8,128)} async-done(((f32[192,1536]{1,0:T(8,128)}), f32[3072,1536]{1,0:T(8,128)}) %all-gather.6.cloned.1.call-update) | async-done | bytes 18874384 | tf_op jit(solution)/shard_map/all_gather | solution.py:32
  148.8 15.9 %fusion.2 = f32[192,1536]{1,0:T(8,128)S(1)} fusion(f32[192,3072]{1,0:T(8,128)S(1)} %bitcast.16, f32[3072,1536]{1,0:T(8,128)} %all-gather.6.cloned.1.call-done), kind=kOutput, calls=%fused_computation.5 | convolution fusion | flops 10871635968 | bytes 22413312 | tf_op jit(solution)/shard_map/dot_general | solution.py:13
  164.8 21.7 %all-gather.8.cloned.1.call-done = f32[192,3072]{1,0:T(8,128)} async-done(((f32[192,1536]{1,0:T(8,128)}), f32[192,3072]{1,0:T(8,128)}) %all-gather.8.cloned.1.call-update) | async-done | bytes 2359312 | tf_op jit(solution)/shard_map/all_gather | solution.py:29
  186.5 19.5 %convolution_bitcast_fusion = f32[3072,1536]{0,1:T(8,128)} fusion(f32[192,1536]{1,0:T(8,128)S(1)} %fusion.2, f32[192,3072]{1,0:T(8,128)} %all-gather.8.cloned.1.call-done), kind=kOutput, calls=%fused_computation | convolution fusion | flops 10871635968 | bytes 22413312 | tf_op jit(solution)/shard_map/dot_general | solution.py:17
  206.0 18.7 %copy.23 = f32[3072,1536]{1,0:T(8,128)} copy(f32[3072,1536]{0,1:T(8,128)} %convolution_bitcast_fusion) | data formatting | bytes 37748736
  225.0 1.0 copy-done.3
  226.0 0.5 copy.17
  226.4 1.7 copy.19
  228.2 190.7 %reduce-scatter.7.cloned.1.call-done = f32[192,1536]{1,0:T(8,128)} async-done(((f32[3072,1536]{1,0:T(8,128)}), f32[192,1536]{1,0:T(8,128)}) %reduce-scatter.7.cloned.1.call-update) | async-done | bytes 1179664
  418.9 3.0 copy.24
  421.9 4.1 add_divide_fusion
  426.0 3.0 copy.20
  429.1 98.1 %all-gather.10.cloned.1.call-done = f32[3072,1536]{1,0:T(8,128)} async-done(((f32[192,1536]{1,0:T(8,128)}), f32[3072,1536]{1,0:T(8,128)}) %all-gather.10.cloned.1.call-update) | async-done | bytes 18874384 | tf_op jit(solution)/shard_map/all_gather | solution.py:45
  527.2 16.5 %fusion.3 = f32[1536,192]{0,1:T(8,128)S(1)} fusion(f32[3072,1536]{1,0:T(8,128)} %all-gather.10.cloned.1.call-done, f32[192,3072]{1,0:T(8,128)S(1)} %copy-done), kind=kOutput, calls=%fused_computation.6 | convolution fusion | flops 10871635968 | bytes 22413312 | tf_op jit(solution)/shard_map/dot_general | solution.py:13
  543.8 23.1 %fusion.4 = f32[192,3072]{1,0:T(8,128)} fusion(f32[1536,192]{0,1:T(8,128)S(1)} %fusion.3, f32[3072,1536]{1,0:T(8,128)} %all-gather.6.cloned.1.call-done), kind=kOutput, calls=%fused_computation.7 | convolution fusion | flops 10871635968 | bytes 22413312 | tf_op jit(solution)/shard_map/dot_general | solution.py:17
  567.0 1.4 copy-done.2
  568.3 1.5 copy.21
  569.8 1.5 copy.22
  571.3 30.6 %reduce-scatter.5.cloned.1.call-done = f32[192,1536]{1,0:T(8,128)} async-done(((f32[192,3072]{1,0:T(8,128)}), f32[192,1536]{1,0:T(8,128)}) %reduce-scatter.5.cloned.1.call-update) | async-done | bytes 1179664 | tf_op jit(solution)/shard_map/reduce_scatter | solution.py:47
  (16 shorter events, 0.9 us)
Async XLA Ops:
  7.2 41.2 %all-gather.12.cloned.1.call-start = ((), (), s32[]{:S(2)}) async-start(), calls=%async_computation.6 | async-start | bytes 3538944 | tf_op jit(solution)/shard_map/all_gather | solution.py:28
  7.9 140.9 %all-gather.6.cloned.1.call-start = ((), (), s32[]{:S(2)}) async-start(), calls=%async_computation.2 | async-start | bytes 20054016 | tf_op jit(solution)/shard_map/all_gather | solution.py:32
  8.6 177.8 %all-gather.8.cloned.1.call-start = ((), (), s32[]{:S(2)}) async-start(), calls=%async_computation.3 | async-start | bytes 3538944 | tf_op jit(solution)/shard_map/all_gather | solution.py:29
  9.4 409.5 %reduce-scatter.7.cloned.1.call-start = ((), (), s32[]{:S(2)}) async-start(), calls=%async_computation.7 | async-start | bytes 20054016
  224.7 1.3 copy-start.3
  224.7 302.5 %all-gather.10.cloned.1.call-start = ((), (), s32[]{:S(2)}) async-start(), calls=%async_computation.4 | async-start | bytes 20054016 | tf_op jit(solution)/shard_map/all_gather | solution.py:45
  426.0 101.2 %copy-start = (f32[192,3072]{1,0:T(8,128)S(1)}, f32[192,3072]{1,0:T(8,128)}, u32[]{:S(2)}) copy-start(f32[192,3072]{1,0:T(8,128)} %all-gather.8.cloned.1.call-done) | copy-start | bytes 7077892
  429.1 172.8 %reduce-scatter.5.cloned.1.call-start = ((), (), s32[]{:S(2)}) async-start(), calls=%async_computation.5 | async-start | bytes 3538944 | tf_op jit(solution)/shard_map/reduce_scatter | solution.py:47
  566.9 1.4 copy-start.2
  566.9 2.9 copy-start.1
Sparse Core Ops, SparseCore 0:
  9.5 38.7 all-gather.11
  49.9 98.8 all-gather.5
  150.4 36.0 all-gather.7
  224.9 194.0 reduce-scatter.6
  429.2 98.0 all-gather.9
  567.1 34.7 reduce-scatter.4
